TPU v7x, 32 devices: a whole 2x2x4 slice. The times are simulated.
32 devices in a mesh: head: 8 (over z, y), ctx: 4 (over x, core).
Axes of the slice: x: 2, y: 2, z: 4, core: 2. Of those that a mesh axis runs over, the one named last changes fastest.
Arguments:
- query: bfloat16 [3072, 4096], P(('ctx', 'head')), may hold values from -8 to 8
- key: bfloat16 [3072, 2048], P(('ctx', 'head')), may hold values from -8 to 8
- value: bfloat16 [3072, 2048], P(('ctx', 'head')), may hold values from -8 to 8
- block_order: int32 [8], replicated, may hold values from 0 to 7, each once
Outputs:
- attended: bfloat16 [3072, 4096], P('ctx', 'head')
Inputs may be any that keep to these rules, and one draw needn't show every extreme that they name: `block_order`: each storage block index 0 to 7 appears exactly once.
All inputs are finite; a program needn't handle non-finite values.
Results may differ from a plain program's by a relative error of at most 0.0049.
Values may be sent and summed in bfloat16 or wider, within the bound.
A program may use at most 128 MiB of HBM per device.

v0:
```python
import jax
import jax.numpy as jnp
from jax import lax
from jax.sharding import PartitionSpec as P

HEAD_WIDTH = 128
query_scale = 1.0 / 12.0
softcap_limit = 50.0


def from_behind(value, axis, by):
    size = lax.axis_size(axis)
    return lax.ppermute(value, axis, [(i, (i + by) % size) for i in range(size)])


def block_pos(block_order, which_block, block_len):
    first = lax.dynamic_index_in_dim(block_order, which_block, 0, keepdims=False)
    return first * block_len + lax.iota(jnp.int32, block_len)


def add_block(totals, query_rows, query_pos, key_block, value_block, key_pos):
    numerator, denominator = totals
    scores = (
        jnp.einsum("rhgd,khd->hgrk", query_rows, key_block, preferred_element_type=jnp.float32)
        * query_scale
    )
    capped = softcap_limit * jnp.tanh(scores / softcap_limit)
    visible = key_pos[None, :] <= query_pos[:, None]
    weights = jnp.where(visible[None, None], jnp.exp(capped), jnp.zeros_like(capped))
    denominator = denominator + jnp.sum(weights, axis=-1)
    numerator = numerator + jnp.einsum(
        "hgrk,khd->rhgd",
        weights.astype(jnp.bfloat16),
        value_block,
        preferred_element_type=jnp.float32,
    )
    return (numerator, denominator)


def shards(query, key, value, block_order):
    query, key, value = (
        lax.all_to_all(query, "head", split_axis=1, concat_axis=0, tiled=True),
        lax.all_to_all(key, "head", split_axis=1, concat_axis=0, tiled=True),
        lax.all_to_all(value, "head", split_axis=1, concat_axis=0, tiled=True),
    )
    row_count = query.shape[0]
    block_len = row_count // 2
    kv_heads = key.shape[1] // HEAD_WIDTH
    group_size = query.shape[1] // key.shape[1]
    query_rows = query.reshape(row_count, kv_heads, group_size, HEAD_WIDTH)
    kv_pair = jnp.stack(
        [
            key.reshape(row_count, kv_heads, HEAD_WIDTH),
            value.reshape(row_count, kv_heads, HEAD_WIDTH),
        ]
    )
    cycle_size = lax.axis_size("ctx")
    cycle_index = lax.axis_index("ctx")
    query_pos = jnp.concatenate(
        [
            block_pos(block_order, 2 * cycle_index, block_len),
            block_pos(block_order, 2 * cycle_index + 1, block_len),
        ]
    )
    start_totals = (
        jnp.zeros((row_count, kv_heads, group_size, HEAD_WIDTH), jnp.float32),
        jnp.zeros((kv_heads, group_size, row_count), jnp.float32),
    )

    def add_shard(totals, held, source):
        for which_half in range(2):
            lower = which_half * block_len
            key_pos = block_pos(block_order, 2 * source + which_half, block_len)
            totals = add_block(
                totals,
                query_rows,
                query_pos,
                held[0, lower : lower + block_len],
                held[1, lower : lower + block_len],
                key_pos,
            )
        return totals

    totals = add_shard(start_totals, kv_pair, cycle_index)

    def from_lower(held):
        return from_behind(held, "ctx", 1)

    def turn_both(turn_index, state):
        forward_kv, backward_kv, sums = state
        forward_kv = from_lower(forward_kv)
        backward_kv = from_behind(backward_kv, "ctx", -1)
        sums = add_shard(sums, forward_kv, (cycle_index - turn_index) % cycle_size)
        sums = add_shard(sums, backward_kv, (cycle_index + turn_index) % cycle_size)
        return (forward_kv, backward_kv, sums)

    forward_kv, backward_kv, totals = lax.fori_loop(
        1, cycle_size // 2, turn_both, (kv_pair, kv_pair, totals)
    )
    forward_kv = from_lower(forward_kv)
    totals = add_shard(totals, forward_kv, (cycle_index + cycle_size // 2) % cycle_size)
    numerator, denominator = totals
    result = numerator / jnp.transpose(denominator, (2, 0, 1))[..., None]
    return result.reshape(row_count, kv_heads * group_size * HEAD_WIDTH).astype(jnp.bfloat16)


def solution(mesh):
    placed = (P(("ctx", "head"), None), P(("ctx", "head"), None), P(("ctx", "head"), None), P())
    return jax.shard_map(
        shards, mesh=mesh, in_specs=placed, out_specs=P("ctx", "head"), check_vma=False
    )
```

profile of v0, /device:TPU:1, one launch (start us, length us, event | category | flops | bytes accessed | tf_op | source)
XLA Modules:
  0.0 99.2 jit_solution(4919566508490505928)
XLA Ops:
  1.8 6.4 %all-to-all-start = ((bf16[96,8,256]{2,0,1:T(8,128)(2,1)}), bf16[96,8,256]{2,0,1:T(8,128)(2,1)S(1)}, u32[]{:S(2)}, u32[]{:S(2)}) async-start(bf16[96,8,256]{2,0,1:T(8,128)(2,1)} %bitcast.228), calls=%async_computation | async-start | bytes 786432 | tf_op jit(solution)/shard_map/all_to_all | solution.py:43
  9.9 7.4 %all-to-all-done = bf16[96,8,256]{2,0,1:T(8,128)(2,1)S(1)} async-done(((bf16[96,8,256]{2,0,1:T(8,128)(2,1)}), bf16[96,8,256]{2,0,1:T(8,128)(2,1)S(1)}, u32[]{:S(2)}, u32[]{:S(2)}) %all-to-all-start) | async-done | bytes 393248 | tf_op jit(solution)/shard_map/all_to_all | solution.py:43
  17.3 6.1 %all-to-all-start.2 = ((bf16[96,8,256]{2,0,1:T(8,128)(2,1)}), bf16[96,8,256]{2,0,1:T(8,128)(2,1)S(1)}, u32[]{:S(2)}, u32[]{:S(2)}) async-start(bf16[96,8,256]{2,0,1:T(8,128)(2,1)} %bitcast.229), calls=%async_computation.2 | async-start | bytes 786432 | tf_op jit(solution)/shard_map/all_to_all | solution.py:44
  28.8 2.1 %copy.133 = bf16[12,8,8,512]{3,2,0,1:T(8,128)(2,1)} copy(bf16[12,8,8,512]{3,2,1,0:T(8,128)(2,1)} %bitcast.234) | data formatting | bytes 1572864 | tf_op jit(solution)/shard_map/all_to_all | solution.py:42
  32.5 6.1 %all-to-all-start.1 = ((bf16[96,8,512]{2,0,1:T(8,128)(2,1)}), bf16[96,8,512]{2,0,1:T(8,128)(2,1)S(1)}, u32[]{:S(2)}, u32[]{:S(2)}) async-start(bf16[96,8,512]{2,0,1:T(8,128)(2,1)} %bitcast.227), calls=%async_computation.1 | async-start | bytes 1572864 | tf_op jit(solution)/shard_map/all_to_all | solution.py:42
  39.8 2.4 %broadcast_compare_fusion = (pred[768,384]{0,1:T(8,128)(4,1)S(1)}, pred[768,384]{0,1:T(8,128)(4,1)}, pred[768,384]{0,1:T(8,128)(4,1)S(1)}, pred[768,384]{0,1:T(8...) fusion(s32[768]{0:T(1024)S(1)} %pad_add_fusion, ...), kind=kLoop, calls=%fused_computation.49 | loop fusion | flops 2359296 | bytes 2374656 | tf_op jit(solution)/shard_map/le | solution.py:28
  44.0 2.2 %collective-permute-start = (bf16[2,768,2,128]{3,1,2,0:T(8,128)(2,1)}, bf16[2,768,2,128]{3,1,2,0:T(8,128)(2,1)}, u32[]{:S(2)}, u32[]{:S(2)}) collective-permute-start(bf16[2,768,2,128]{3,1,2,0:T(8,128)(2,1)} %copy_dynamic-update-slice_fusion), channel_id=1, source_target_pairs={{0,1},{1,2},{2,3},{3,0},{4,5},{5,6},{6,7},{7,4},{8,9},{9,10},{10,1... | collective-permute-start | bytes 2359304 | tf_op jit(solution)/shard_map/while/body/eval_jaxpr/ppermute | solution.py:13
  46.9 10.7 %all-to-all-done.1 = bf16[96,8,512]{2,0,1:T(8,128)(2,1)S(1)} async-done(((bf16[96,8,512]{2,0,1:T(8,128)(2,1)}), bf16[96,8,512]{2,0,1:T(8,128)(2,1)S(1)}, u32[]{:S(2)}, u32[]{:S(2)}) %all-to-all-start.1) | async-done | bytes 786464 | tf_op jit(solution)/shard_map/all_to_all | solution.py:42
  57.8 2.8 %fusion = (f32[2,2,768]{2,1,0:T(2,128)S(1)}, f32[2,384,768,2]{2,1,3,0:T(8,128)S(1)}) fusion(pred[768,384]{0,1:T(8,128)(4,1)} %get-tuple-element.46, bf16[768,2,2,128]{3,2,1,0:T(2,128)(2,1)S(1)} %reshape.260, bf16[1,768,2,128]{3,1,2,0:T(8,128)(2,1)S(1)} %get-tuple-element.25), kind=kOutput, calls=%fused_computation.8 | convolution fusion | flops 306705408 | bytes 6008832 | tf_op jit(solution)/shard_map/rhgd,khd->hgrk/dot_general | solution.py:24
  60.6 1.8 %fusion.30 = f32[2,2,768,128]{2,3,1,0:T(8,128)S(1)} fusion(f32[2,384,768,2]{2,1,3,0:T(8,128)S(1)} %get-tuple-element.68, pred[768,384]{0,1:T(8,128)(4,1)S(1)} %copy-done.3, bf16[1,384,2,128]{1,3,2,0:T(8,128)(2,1)S(1)} %copy.90), kind=kOutput, calls=%fused_computation.31 | convolution fusion | flops 306708480 | bytes 6782976 | tf_op jit(solution)/shard_map/hgrk,khd->rhgd/dot_general | solution.py:31
  62.4 1.8 %fusion.2 = (f32[2,2,768]{2,1,0:T(2,128)S(1)}, f32[2,384,768,2]{2,1,3,0:T(8,128)S(1)}) fusion(pred[768,384]{0,1:T(8,128)(4,1)S(1)} %copy-done.2, bf16[768,2,2,128]{3,2,1,0:T(2,128)(2,1)S(1)} %reshape.260, bf16[1,768,2,128]{3,1,2,0:T(8,128)(2,1)S(1)} %get-tuple-element.25), kind=kOutput, calls=%fused_computation.10 | convolution fusion | flops 306705408 | bytes 6008832 | tf_op jit(solution)/shard_map/rhgd,khd->hgrk/dot_general | solution.py:24
  64.2 1.8 %fusion.28 = f32[2,2,768,128]{2,3,1,0:T(8,128)S(1)} fusion(f32[2,384,768,2]{2,1,3,0:T(8,128)S(1)} %get-tuple-element.70, pred[768,384]{0,1:T(8,128)(4,1)S(1)} %copy-done.2, bf16[1,384,2,128]{1,3,2,0:T(8,128)(2,1)S(1)} %copy.91), kind=kOutput, calls=%fused_computation.30 | convolution fusion | flops 306708480 | bytes 6782976 | tf_op jit(solution)/shard_map/hgrk,khd->rhgd/dot_general | solution.py:31
  66.0 3.5 %collective-permute-start.2 = (bf16[2,768,2,128]{3,1,2,0:T(8,128)(2,1)}, bf16[2,768,2,128]{3,1,2,0:T(8,128)(2,1)S(1)}, u32[]{:S(2)}, u32[]{:S(2)}) collective-permute-start(bf16[2,768,2,128]{3,1,2,0:T(8,128)(2,1)} %collective-permute-done), channel_id=1, source_target_pairs={{0,1},{1,2},{2,3},{3,0},{4,5},{5,6},{6,7},{7,4},{8,9},{9,10},{10,1... | collective-permute-start | bytes 2359304 | tf_op jit(solution)/shard_map/ppermute | solution.py:13
  69.5 2.7 %fusion.10 = (f32[2,2,768]{2,1,0:T(2,128)S(1)}, f32[2,384,768,2]{2,1,3,0:T(8,128)S(1)}) fusion(pred[768,384]{0,1:T(8,128)(4,1)S(1)} %copy-done.1, bf16[768,2,2,128]{3,2,1,0:T(2,128)(2,1)S(1)} %reshape.260, bf16[2,768,2,128]{3,1,2,0:T(8,128)(2,1)} %collective-permute-done.1), kind=kOutput, calls=%fused_computation.18 | convolution fusion | flops 306705408 | bytes 6008832 | tf_op jit(solution)/shard_map/while/body/eval_jaxpr/rhgd,khd->hgrk/dot_general | solution.py:24
  72.2 2.6 %fusion.20 = f32[2,128,2,768]{3,1,2,0:T(8,128)S(1)} fusion(f32[2,384,768,2]{2,1,3,0:T(8,128)S(1)} %get-tuple-element.60, pred[768,384]{0,1:T(8,128)(4,1)S(1)} %copy-done.1, bf16[2,768,2,128]{3,1,2,0:T(8,128)(2,1)} %collective-permute-done.1), kind=kOutput, calls=%fused_computation.26 | convolution fusion | flops 306708480 | bytes 6782976 | tf_op jit(solution)/shard_map/while/body/eval_jaxpr/hgrk,khd->rhgd/dot_general | solution.py:31
  74.8 2.7 %fusion.8 = (f32[2,2,768]{2,1,0:T(2,128)S(1)}, f32[2,384,768,2]{2,1,3,0:T(8,128)S(1)}) fusion(pred[768,384]{0,1:T(8,128)(4,1)S(1)} %copy-done, bf16[768,2,2,128]{3,2,1,0:T(2,128)(2,1)S(1)} %reshape.260, bf16[2,768,2,128]{3,1,2,0:T(8,128)(2,1)} %collective-permute-done.1), kind=kOutput, calls=%fused_computation.16 | convolution fusion | flops 306705408 | bytes 6008832 | tf_op jit(solution)/shard_map/while/body/eval_jaxpr/rhgd,khd->hgrk/dot_general | solution.py:24
  77.5 2.5 %fusion.22 = f32[2,128,2,768]{3,1,2,0:T(8,128)S(1)} fusion(f32[2,384,768,2]{2,1,3,0:T(8,128)S(1)} %get-tuple-element.62, pred[768,384]{0,1:T(8,128)(4,1)S(1)} %copy-done, bf16[2,768,2,128]{3,1,2,0:T(8,128)(2,1)} %collective-permute-done.1), kind=kOutput, calls=%fused_computation.27 | convolution fusion | flops 306708480 | bytes 6782976 | tf_op jit(solution)/shard_map/while/body/eval_jaxpr/hgrk,khd->rhgd/dot_general | solution.py:31
  80.1 2.7 %fusion.6 = (f32[2,2,768]{2,1,0:T(2,128)S(1)}, f32[2,384,768,2]{2,1,3,0:T(8,128)S(1)}) fusion(pred[768,384]{0,1:T(8,128)(4,1)S(1)} %get-tuple-element.40, bf16[768,2,2,128]{3,2,1,0:T(2,128)(2,1)S(1)} %reshape.260, bf16[2,768,2,128]{3,1,2,0:T(8,128)(2,1)} %collective-permute-done), kind=kOutput, calls=%fused_computation.14 | convolution fusion | flops 306705408 | bytes 6008832 | tf_op jit(solution)/shard_map/while/body/eval_jaxpr/rhgd,khd->hgrk/dot_general | solution.py:24
  82.8 2.5 %fusion.24 = f32[2,128,2,768]{3,1,2,0:T(8,128)S(1)} fusion(f32[2,384,768,2]{2,1,3,0:T(8,128)S(1)} %get-tuple-element.64, pred[768,384]{0,1:T(8,128)(4,1)S(1)} %get-tuple-element.40, bf16[2,768,2,128]{3,1,2,0:T(8,128)(2,1)} %collective-permute-done), kind=kOutput, calls=%fused_computation.28 | convolution fusion | flops 306708480 | bytes 6782976 | tf_op jit(solution)/shard_map/while/body/eval_jaxpr/hgrk,khd->rhgd/dot_general | solution.py:31
  85.3 2.7 %fusion.4 = (f32[2,2,768]{2,1,0:T(2,128)S(1)}, f32[2,384,768,2]{2,1,3,0:T(8,128)S(1)}) fusion(pred[768,384]{0,1:T(8,128)(4,1)S(1)} %get-tuple-element.29, bf16[768,2,2,128]{3,2,1,0:T(2,128)(2,1)S(1)} %reshape.260, bf16[2,768,2,128]{3,1,2,0:T(8,128)(2,1)} %collective-permute-done), kind=kOutput, calls=%fused_computation.12 | convolution fusion | flops 306705408 | bytes 6008832 | tf_op jit(solution)/shard_map/while/body/eval_jaxpr/rhgd,khd->hgrk/dot_general | solution.py:24
  88.1 2.7 %fusion.26 = f32[2,128,2,768]{3,1,2,0:T(8,128)S(1)} fusion(f32[2,384,768,2]{2,1,3,0:T(8,128)S(1)} %get-tuple-element.66, pred[768,384]{0,1:T(8,128)(4,1)S(1)} %get-tuple-element.29, bf16[2,768,2,128]{3,1,2,0:T(8,128)(2,1)} %collective-permute-done), kind=kOutput, calls=%fused_computation.29 | convolution fusion | flops 306708480 | bytes 6782976 | tf_op jit(solution)/shard_map/while/body/eval_jaxpr/hgrk,khd->rhgd/dot_general | solution.py:31
  90.8 1.8 %fusion.12 = (f32[2,2,768]{2,1,0:T(2,128)S(1)}, f32[2,384,768,2]{2,1,3,0:T(8,128)S(1)}) fusion(pred[768,384]{0,1:T(8,128)(4,1)S(1)} %get-tuple-element.45, bf16[768,2,2,128]{3,2,1,0:T(2,128)(2,1)S(1)} %reshape.260, bf16[2,768,2,128]{3,1,2,0:T(8,128)(2,1)S(1)} %collective-permute-done.2), kind=kOutput, calls=%fused_computation.20 | convolution fusion | flops 306705408 | bytes 6008832 | tf_op jit(solution)/shard_map/rhgd,khd->hgrk/dot_general | solution.py:24
  92.6 1.8 %fusion.14 = (f32[2,2,768]{2,1,0:T(2,128)S(1)}, f32[2,384,768,2]{2,1,3,0:T(8,128)S(1)}) fusion(pred[768,384]{0,1:T(8,128)(4,1)S(1)} %get-tuple-element.27, bf16[768,2,2,128]{3,2,1,0:T(2,128)(2,1)S(1)} %reshape.260, bf16[2,768,2,128]{3,1,2,0:T(8,128)(2,1)S(1)} %collective-permute-done.2), kind=kOutput, calls=%fused_computation.22 | convolution fusion | flops 306705408 | bytes 6008832 | tf_op jit(solution)/shard_map/rhgd,khd->hgrk/dot_general | solution.py:24
  96.1 2.0 %fusion.41 = bf16[768,2,2,128]{0,3,2,1:T(8,128)(2,1)S(1)} fusion(f32[2,128,2,768]{3,1,2,0:T(8,128)S(1)} %fusion.18, f32[2,128,2,768]{3,1,2,0:T(8,128)S(1)} %fusion.20, f32[2,128,2,768]{3,1,2,0:T(8,128)S(1)} %fusion.22, f32[2,128,2,768]{3,1,2,0:T(8,128)S(1)} %fusion.24, f32[2,128,2,768]{3,1,2,0:T(8,128)S(1)} %fusion.26, f32[2,2,768,128]{2,3,1,0:T(8,128)S(1)} %fusion.30, ...), kind=kOutput, calls=%fused_computation.42 | convolution fusion | flops 310247424 | bytes 17018880 | tf_op jit(solution)/shard_map/hgrk,khd->rhgd/dot_general | solution.py:31
  (32 shorter events, 12.3 us)
Async XLA Ops:
  1.8 15.5 %all-to-all-start = ((bf16[96,8,256]{2,0,1:T(8,128)(2,1)}), bf16[96,8,256]{2,0,1:T(8,128)(2,1)S(1)}, u32[]{:S(2)}, u32[]{:S(2)}) async-start(bf16[96,8,256]{2,0,1:T(8,128)(2,1)} %bitcast.228), calls=%async_computation | async-start | bytes 786432 | tf_op jit(solution)/shard_map/all_to_all | solution.py:43
  17.3 15.2 %all-to-all-start.2 = ((bf16[96,8,256]{2,0,1:T(8,128)(2,1)}), bf16[96,8,256]{2,0,1:T(8,128)(2,1)S(1)}, u32[]{:S(2)}, u32[]{:S(2)}) async-start(bf16[96,8,256]{2,0,1:T(8,128)(2,1)} %bitcast.229), calls=%async_computation.2 | async-start | bytes 786432 | tf_op jit(solution)/shard_map/all_to_all | solution.py:44
  32.5 25.1 %all-to-all-start.1 = ((bf16[96,8,512]{2,0,1:T(8,128)(2,1)}), bf16[96,8,512]{2,0,1:T(8,128)(2,1)S(1)}, u32[]{:S(2)}, u32[]{:S(2)}) async-start(bf16[96,8,512]{2,0,1:T(8,128)(2,1)} %bitcast.227), calls=%async_computation.1 | async-start | bytes 1572864 | tf_op jit(solution)/shard_map/all_to_all | solution.py:42
  44.0 22.0 %collective-permute-start = (bf16[2,768,2,128]{3,1,2,0:T(8,128)(2,1)}, bf16[2,768,2,128]{3,1,2,0:T(8,128)(2,1)}, u32[]{:S(2)}, u32[]{:S(2)}) collective-permute-start(bf16[2,768,2,128]{3,1,2,0:T(8,128)(2,1)} %copy_dynamic-update-slice_fusion), channel_id=1, source_target_pairs={{0,1},{1,2},{2,3},{3,0},{4,5},{5,6},{6,7},{7,4},{8,9},{9,10},{10,1... | collective-permute-start | bytes 2359304 | tf_op jit(solution)/shard_map/while/body/eval_jaxpr/ppermute | solution.py:13
  46.3 23.2 %collective-permute-start.1 = (bf16[2,768,2,128]{3,1,2,0:T(8,128)(2,1)}, bf16[2,768,2,128]{3,1,2,0:T(8,128)(2,1)}, u32[]{:S(2)}, u32[]{:S(2)}) collective-permute-start(bf16[2,768,2,128]{3,1,2,0:T(8,128)(2,1)} %copy_dynamic-update-slice_fusion), channel_id=1, source_target_pairs={{0,3},{1,0},{2,1},{3,2},{4,7},{5,4},{6,5},{7,6},{8,11},{9,8},{10,9... | collective-permute-start | bytes 2359304 | tf_op jit(solution)/shard_map/while/body/eval_jaxpr/ppermute | solution.py:13
  57.8 2.8 %copy-start.3 = (pred[768,384]{0,1:T(8,128)(4,1)S(1)}, pred[768,384]{0,1:T(8,128)(4,1)}, u32[]{:S(2)}) copy-start(pred[768,384]{0,1:T(8,128)(4,1)} %get-tuple-element.46) | copy-start | bytes 884740
  60.6 1.8 %copy-start.2 = (pred[768,384]{0,1:T(8,128)(4,1)S(1)}, pred[768,384]{0,1:T(8,128)(4,1)}, u32[]{:S(2)}) copy-start(pred[768,384]{0,1:T(8,128)(4,1)} %get-tuple-element.28) | copy-start | bytes 884740
  64.2 5.3 %copy-start.1 = (pred[768,384]{0,1:T(8,128)(4,1)S(1)}, pred[768,384]{0,1:T(8,128)(4,1)}, u32[]{:S(2)}) copy-start(pred[768,384]{0,1:T(8,128)(4,1)} %get-tuple-element.44) | copy-start | bytes 884740
  66.0 24.8 %collective-permute-start.2 = (bf16[2,768,2,128]{3,1,2,0:T(8,128)(2,1)}, bf16[2,768,2,128]{3,1,2,0:T(8,128)(2,1)S(1)}, u32[]{:S(2)}, u32[]{:S(2)}) collective-permute-start(bf16[2,768,2,128]{3,1,2,0:T(8,128)(2,1)} %collective-permute-done), channel_id=1, source_target_pairs={{0,1},{1,2},{2,3},{3,0},{4,5},{5,6},{6,7},{7,4},{8,9},{9,10},{10,1... | collective-permute-start | bytes 2359304 | tf_op jit(solution)/shard_map/ppermute | solution.py:13
  72.2 2.6 %copy-start = (pred[768,384]{0,1:T(8,128)(4,1)S(1)}, pred[768,384]{0,1:T(8,128)(4,1)}, u32[]{:S(2)}) copy-start(pred[768,384]{0,1:T(8,128)(4,1)} %get-tuple-element.42) | copy-start | bytes 884740
where the time goes:
time: 100 us; the launch traced here: 99.2 us
  matrix products  36.6 us (37%)
  starting transfers between devices  24.2 us (24%)
  waiting for transfers between devices  19.7 us (20%)
  local copies, waits for them, and re-layouts  11.1 us (11%)
  between operations  5.27 us (5%)
  other arithmetic  2.43 us (2%)
    dot_general x8, matrix products, add_block(): jnp.einsum('rhgd,khd->hgrk', query_rows, key_block, preferred_element_typ...  19 us
    dot_general x8, matrix products, add_block(): jnp.einsum('hgrk,khd->rhgd', weights.astype(jnp.bfloat16), value_block, p...  17.6 us
    all_to_all x1, waiting for transfers between devices, shards(): lax.all_to_all(query, 'head', split_axis=1, concat_axis=0, tiled=True)  10.7 us
    all_to_all x1, waiting for transfers between devices, shards(): lax.all_to_all(key, 'head', split_axis=1, concat_axis=0, tiled=True)  7.41 us
    all_to_all x1, starting transfers between devices, shards(): lax.all_to_all(key, 'head', split_axis=1, concat_axis=0, tiled=True)  6.37 us
    all_to_all x1, starting transfers between devices, shards(): lax.all_to_all(query, 'head', split_axis=1, concat_axis=0, tiled=True)  6.06 us
    all_to_all x1, starting transfers between devices, shards(): lax.all_to_all(value, 'head', split_axis=1, concat_axis=0, tiled=True)  6.06 us
    ppermute x3, starting transfers between devices, from_behind(): lax.ppermute(value, axis, [(i, (i + by) % size) for i in range(size)])  5.67 us
  transfers between devices with their start and end apart: 6, of which 3 were waited for; matrix products, arithmetic and copies ran while one was open for 40% of the time, Pallas kernels for 0%

commit v1 on v0

--- a/solution.py
+++ b/solution.py
@@ -40,7 +40,10 @@
 def shards(query, key, value, block_order):
     query, key, value = (
         lax.all_to_all(query, "head", split_axis=1, concat_axis=0, tiled=True),
-        lax.all_to_all(key, "head", split_axis=1, concat_axis=0, tiled=True),
+        jnp.concatenate(
+            lax.all_to_all(jnp.stack(jnp.split(key, lax.axis_size("head"), axis=1)), "head", 0, 0),
+            axis=0,
+        ),
         lax.all_to_all(value, "head", split_axis=1, concat_axis=0, tiled=True),
     )
     row_count = query.shape[0]

time: 100 us -> 110 us (1.10)
  local copies, waits for them, and re-layouts: 11.1 us -> 20.7 us
    unnamed x10 -> x17, local copies, waits for them, and re-layouts: 0.37 us -> 10.3 us
    all_to_all x1 -> x0, local copies, waits for them, and re-layouts: 1.77 us -> none  [shards(): lax.all_to_all(key, 'head', split_axis=1, concat_axis=0, tiled=True)]
    another operation x0 -> x1, local copies, waits for them, and re-layouts: none -> 1.42 us  [shards(): jnp.stack(jnp.split(key, lax.axis_size('head'), axis=1))]
  transfers between devices with their start and end apart: 6 -> 6, of which waited for: 3 -> 3; matrix products, arithmetic and copies ran while one was open for 40% -> 37% of each run, Pallas kernels for 0% -> 0%
where the time goes in v1:
time: 110 us; the launch traced here: 109 us
  matrix products  36.6 us (33%)
  starting transfers between devices  24.2 us (22%)
  local copies, waits for them, and re-layouts  20.7 us (19%)
  waiting for transfers between devices  19.7 us (18%)
  between operations  5.27 us (5%)
  other arithmetic  2.43 us (2%)
    dot_general x8, matrix products, add_block(): jnp.einsum('rhgd,khd->hgrk', query_rows, key_block, preferred_element_typ...  19 us
    dot_general x8, matrix products, add_block(): jnp.einsum('hgrk,khd->rhgd', weights.astype(jnp.bfloat16), value_block, p...  17.6 us
    all_to_all x1, waiting for transfers between devices, shards(): lax.all_to_all(query, 'head', split_axis=1, concat_axis=0, tiled=True)  10.7 us
    unnamed x17, local copies, waits for them, and re-layouts  10.3 us
    all_to_all x1, waiting for transfers between devices, shards(): lax.all_to_all(jnp.stack(jnp.split(key, lax.axis_size('head'), axis=1)),...  7.41 us
    all_to_all x1, starting transfers between devices, shards(): lax.all_to_all(jnp.stack(jnp.split(key, lax.axis_size('head'), axis=1)),...  6.37 us
    all_to_all x1, starting transfers between devices, shards(): lax.all_to_all(query, 'head', split_axis=1, concat_axis=0, tiled=True)  6.06 us
    all_to_all x1, starting transfers between devices, shards(): lax.all_to_all(value, 'head', split_axis=1, concat_axis=0, tiled=True)  6.06 us
  transfers between devices with their start and end apart: 6, of which 3 were waited for; matrix products, arithmetic and copies ran while one was open for 37% of the time, Pallas kernels for 0%

profile of v1, /device:TPU:1, one launch (start us, length us, event | category | flops | bytes accessed | tf_op | source)
XLA Modules:
  0.0 108.8 jit_solution(4893535403671913944)
XLA Ops:
  11.4 6.4 %all-to-all-start = ((bf16[8,96,256]{2,1,0:T(8,128)(2,1)}), bf16[8,96,256]{2,1,0:T(8,128)(2,1)S(1)}, u32[]{:S(2)}, u32[]{:S(2)}) async-start(bf16[8,96,256]{2,1,0:T(8,128)(2,1)} %bitcast_dynamic-update-slice_fusion), calls=%async_computation | async-start | bytes 786432 | tf_op jit(solution)/shard_map/all_to_all | solution.py:44
  19.5 7.4 %all-to-all-done = bf16[8,96,256]{2,1,0:T(8,128)(2,1)S(1)} async-done(((bf16[8,96,256]{2,1,0:T(8,128)(2,1)}), bf16[8,96,256]{2,1,0:T(8,128)(2,1)S(1)}, u32[]{:S(2)}, u32[]{:S(2)}) %all-to-all-start) | async-done | bytes 393248 | tf_op jit(solution)/shard_map/all_to_all | solution.py:44
  26.9 6.1 %all-to-all-start.2 = ((bf16[96,8,256]{2,0,1:T(8,128)(2,1)}), bf16[96,8,256]{2,0,1:T(8,128)(2,1)S(1)}, u32[]{:S(2)}, u32[]{:S(2)}) async-start(bf16[96,8,256]{2,0,1:T(8,128)(2,1)} %bitcast.240), calls=%async_computation.2 | async-start | bytes 786432 | tf_op jit(solution)/shard_map/all_to_all | solution.py:47
  38.4 2.1 %copy.130 = bf16[12,8,8,512]{3,2,0,1:T(8,128)(2,1)} copy(bf16[12,8,8,512]{3,2,1,0:T(8,128)(2,1)} %bitcast.244) | data formatting | bytes 1572864 | tf_op jit(solution)/shard_map/all_to_all | solution.py:42
  42.1 6.1 %all-to-all-start.1 = ((bf16[96,8,512]{2,0,1:T(8,128)(2,1)}), bf16[96,8,512]{2,0,1:T(8,128)(2,1)S(1)}, u32[]{:S(2)}, u32[]{:S(2)}) async-start(bf16[96,8,512]{2,0,1:T(8,128)(2,1)} %bitcast.239), calls=%async_computation.1 | async-start | bytes 1572864 | tf_op jit(solution)/shard_map/all_to_all | solution.py:42
  49.4 2.4 %broadcast_compare_fusion = (pred[768,384]{0,1:T(8,128)(4,1)S(1)}, pred[768,384]{0,1:T(8,128)(4,1)}, pred[768,384]{0,1:T(8,128)(4,1)S(1)}, pred[768,384]{0,1:T(8...) fusion(s32[768]{0:T(1024)S(1)} %pad_add_fusion, ...), kind=kLoop, calls=%fused_computation.49 | loop fusion | flops 2359296 | bytes 2374656 | tf_op jit(solution)/shard_map/le | solution.py:28
  53.6 2.2 %collective-permute-start = (bf16[2,768,2,128]{3,1,2,0:T(8,128)(2,1)}, bf16[2,768,2,128]{3,1,2,0:T(8,128)(2,1)}, u32[]{:S(2)}, u32[]{:S(2)}) collective-permute-start(bf16[2,768,2,128]{3,1,2,0:T(8,128)(2,1)} %copy_dynamic-update-slice_fusion), channel_id=1, source_target_pairs={{0,1},{1,2},{2,3},{3,0},{4,5},{5,6},{6,7},{7,4},{8,9},{9,10},{10,1... | collective-permute-start | bytes 2359304 | tf_op jit(solution)/shard_map/while/body/eval_jaxpr/ppermute | solution.py:13
  56.5 10.7 %all-to-all-done.1 = bf16[96,8,512]{2,0,1:T(8,128)(2,1)S(1)} async-done(((bf16[96,8,512]{2,0,1:T(8,128)(2,1)}), bf16[96,8,512]{2,0,1:T(8,128)(2,1)S(1)}, u32[]{:S(2)}, u32[]{:S(2)}) %all-to-all-start.1) | async-done | bytes 786464 | tf_op jit(solution)/shard_map/all_to_all | solution.py:42
  67.4 2.8 %fusion = (f32[2,2,768]{2,1,0:T(2,128)S(1)}, f32[2,384,768,2]{2,1,3,0:T(8,128)S(1)}) fusion(pred[768,384]{0,1:T(8,128)(4,1)} %get-tuple-element.46, bf16[768,2,2,128]{3,2,1,0:T(2,128)(2,1)S(1)} %reshape.256, bf16[1,768,2,128]{3,1,2,0:T(8,128)(2,1)S(1)} %get-tuple-element.25), kind=kOutput, calls=%fused_computation.8 | convolution fusion | flops 306705408 | bytes 6008832 | tf_op jit(solution)/shard_map/rhgd,khd->hgrk/dot_general | solution.py:24
  70.2 1.8 %fusion.30 = f32[2,2,768,128]{2,3,1,0:T(8,128)S(1)} fusion(f32[2,384,768,2]{2,1,3,0:T(8,128)S(1)} %get-tuple-element.68, pred[768,384]{0,1:T(8,128)(4,1)S(1)} %copy-done.3, bf16[1,384,2,128]{1,3,2,0:T(8,128)(2,1)S(1)} %copy.89), kind=kOutput, calls=%fused_computation.31 | convolution fusion | flops 306708480 | bytes 6782976 | tf_op jit(solution)/shard_map/hgrk,khd->rhgd/dot_general | solution.py:31
  72.0 1.8 %fusion.2 = (f32[2,2,768]{2,1,0:T(2,128)S(1)}, f32[2,384,768,2]{2,1,3,0:T(8,128)S(1)}) fusion(pred[768,384]{0,1:T(8,128)(4,1)S(1)} %copy-done.2, bf16[768,2,2,128]{3,2,1,0:T(2,128)(2,1)S(1)} %reshape.256, bf16[1,768,2,128]{3,1,2,0:T(8,128)(2,1)S(1)} %get-tuple-element.25), kind=kOutput, calls=%fused_computation.10 | convolution fusion | flops 306705408 | bytes 6008832 | tf_op jit(solution)/shard_map/rhgd,khd->hgrk/dot_general | solution.py:24
  73.8 1.8 %fusion.28 = f32[2,2,768,128]{2,3,1,0:T(8,128)S(1)} fusion(f32[2,384,768,2]{2,1,3,0:T(8,128)S(1)} %get-tuple-element.70, pred[768,384]{0,1:T(8,128)(4,1)S(1)} %copy-done.2, bf16[1,384,2,128]{1,3,2,0:T(8,128)(2,1)S(1)} %copy.90), kind=kOutput, calls=%fused_computation.30 | convolution fusion | flops 306708480 | bytes 6782976 | tf_op jit(solution)/shard_map/hgrk,khd->rhgd/dot_general | solution.py:31
  75.6 3.5 %collective-permute-start.2 = (bf16[2,768,2,128]{3,1,2,0:T(8,128)(2,1)}, bf16[2,768,2,128]{3,1,2,0:T(8,128)(2,1)S(1)}, u32[]{:S(2)}, u32[]{:S(2)}) collective-permute-start(bf16[2,768,2,128]{3,1,2,0:T(8,128)(2,1)} %collective-permute-done), channel_id=1, source_target_pairs={{0,1},{1,2},{2,3},{3,0},{4,5},{5,6},{6,7},{7,4},{8,9},{9,10},{10,1... | collective-permute-start | bytes 2359304 | tf_op jit(solution)/shard_map/ppermute | solution.py:13
  79.1 2.7 %fusion.10 = (f32[2,2,768]{2,1,0:T(2,128)S(1)}, f32[2,384,768,2]{2,1,3,0:T(8,128)S(1)}) fusion(pred[768,384]{0,1:T(8,128)(4,1)S(1)} %copy-done.1, bf16[768,2,2,128]{3,2,1,0:T(2,128)(2,1)S(1)} %reshape.256, bf16[2,768,2,128]{3,1,2,0:T(8,128)(2,1)} %collective-permute-done.1), kind=kOutput, calls=%fused_computation.18 | convolution fusion | flops 306705408 | bytes 6008832 | tf_op jit(solution)/shard_map/while/body/eval_jaxpr/rhgd,khd->hgrk/dot_general | solution.py:24
  81.8 2.6 %fusion.20 = f32[2,128,2,768]{3,1,2,0:T(8,128)S(1)} fusion(f32[2,384,768,2]{2,1,3,0:T(8,128)S(1)} %get-tuple-element.60, pred[768,384]{0,1:T(8,128)(4,1)S(1)} %copy-done.1, bf16[2,768,2,128]{3,1,2,0:T(8,128)(2,1)} %collective-permute-done.1), kind=kOutput, calls=%fused_computation.26 | convolution fusion | flops 306708480 | bytes 6782976 | tf_op jit(solution)/shard_map/while/body/eval_jaxpr/hgrk,khd->rhgd/dot_general | solution.py:31
  84.4 2.7 %fusion.8 = (f32[2,2,768]{2,1,0:T(2,128)S(1)}, f32[2,384,768,2]{2,1,3,0:T(8,128)S(1)}) fusion(pred[768,384]{0,1:T(8,128)(4,1)S(1)} %copy-done, bf16[768,2,2,128]{3,2,1,0:T(2,128)(2,1)S(1)} %reshape.256, bf16[2,768,2,128]{3,1,2,0:T(8,128)(2,1)} %collective-permute-done.1), kind=kOutput, calls=%fused_computation.16 | convolution fusion | flops 306705408 | bytes 6008832 | tf_op jit(solution)/shard_map/while/body/eval_jaxpr/rhgd,khd->hgrk/dot_general | solution.py:24
  87.1 2.5 %fusion.22 = f32[2,128,2,768]{3,1,2,0:T(8,128)S(1)} fusion(f32[2,384,768,2]{2,1,3,0:T(8,128)S(1)} %get-tuple-element.62, pred[768,384]{0,1:T(8,128)(4,1)S(1)} %copy-done, bf16[2,768,2,128]{3,1,2,0:T(8,128)(2,1)} %collective-permute-done.1), kind=kOutput, calls=%fused_computation.27 | convolution fusion | flops 306708480 | bytes 6782976 | tf_op jit(solution)/shard_map/while/body/eval_jaxpr/hgrk,khd->rhgd/dot_general | solution.py:31
  89.7 2.7 %fusion.6 = (f32[2,2,768]{2,1,0:T(2,128)S(1)}, f32[2,384,768,2]{2,1,3,0:T(8,128)S(1)}) fusion(pred[768,384]{0,1:T(8,128)(4,1)S(1)} %get-tuple-element.40, bf16[768,2,2,128]{3,2,1,0:T(2,128)(2,1)S(1)} %reshape.256, bf16[2,768,2,128]{3,1,2,0:T(8,128)(2,1)} %collective-permute-done), kind=kOutput, calls=%fused_computation.14 | convolution fusion | flops 306705408 | bytes 6008832 | tf_op jit(solution)/shard_map/while/body/eval_jaxpr/rhgd,khd->hgrk/dot_general | solution.py:24
  92.4 2.5 %fusion.24 = f32[2,128,2,768]{3,1,2,0:T(8,128)S(1)} fusion(f32[2,384,768,2]{2,1,3,0:T(8,128)S(1)} %get-tuple-element.64, pred[768,384]{0,1:T(8,128)(4,1)S(1)} %get-tuple-element.40, bf16[2,768,2,128]{3,1,2,0:T(8,128)(2,1)} %collective-permute-done), kind=kOutput, calls=%fused_computation.28 | convolution fusion | flops 306708480 | bytes 6782976 | tf_op jit(solution)/shard_map/while/body/eval_jaxpr/hgrk,khd->rhgd/dot_general | solution.py:31
  94.9 2.7 %fusion.4 = (f32[2,2,768]{2,1,0:T(2,128)S(1)}, f32[2,384,768,2]{2,1,3,0:T(8,128)S(1)}) fusion(pred[768,384]{0,1:T(8,128)(4,1)S(1)} %get-tuple-element.29, bf16[768,2,2,128]{3,2,1,0:T(2,128)(2,1)S(1)} %reshape.256, bf16[2,768,2,128]{3,1,2,0:T(8,128)(2,1)} %collective-permute-done), kind=kOutput, calls=%fused_computation.12 | convolution fusion | flops 306705408 | bytes 6008832 | tf_op jit(solution)/shard_map/while/body/eval_jaxpr/rhgd,khd->hgrk/dot_general | solution.py:24
  97.6 2.7 %fusion.26 = f32[2,128,2,768]{3,1,2,0:T(8,128)S(1)} fusion(f32[2,384,768,2]{2,1,3,0:T(8,128)S(1)} %get-tuple-element.66, pred[768,384]{0,1:T(8,128)(4,1)S(1)} %get-tuple-element.29, bf16[2,768,2,128]{3,1,2,0:T(8,128)(2,1)} %collective-permute-done), kind=kOutput, calls=%fused_computation.29 | convolution fusion | flops 306708480 | bytes 6782976 | tf_op jit(solution)/shard_map/while/body/eval_jaxpr/hgrk,khd->rhgd/dot_general | solution.py:31
  100.4 1.8 %fusion.12 = (f32[2,2,768]{2,1,0:T(2,128)S(1)}, f32[2,384,768,2]{2,1,3,0:T(8,128)S(1)}) fusion(pred[768,384]{0,1:T(8,128)(4,1)S(1)} %get-tuple-element.45, bf16[768,2,2,128]{3,2,1,0:T(2,128)(2,1)S(1)} %reshape.256, bf16[2,768,2,128]{3,1,2,0:T(8,128)(2,1)S(1)} %collective-permute-done.2), kind=kOutput, calls=%fused_computation.20 | convolution fusion | flops 306705408 | bytes 6008832 | tf_op jit(solution)/shard_map/rhgd,khd->hgrk/dot_general | solution.py:24
  102.2 1.8 %fusion.14 = (f32[2,2,768]{2,1,0:T(2,128)S(1)}, f32[2,384,768,2]{2,1,3,0:T(8,128)S(1)}) fusion(pred[768,384]{0,1:T(8,128)(4,1)S(1)} %get-tuple-element.27, bf16[768,2,2,128]{3,2,1,0:T(2,128)(2,1)S(1)} %reshape.256, bf16[2,768,2,128]{3,1,2,0:T(8,128)(2,1)S(1)} %collective-permute-done.2), kind=kOutput, calls=%fused_computation.22 | convolution fusion | flops 306705408 | bytes 6008832 | tf_op jit(solution)/shard_map/rhgd,khd->hgrk/dot_general | solution.py:24
  105.6 2.0 %fusion.41 = bf16[768,2,2,128]{0,3,2,1:T(8,128)(2,1)S(1)} fusion(f32[2,128,2,768]{3,1,2,0:T(8,128)S(1)} %fusion.18, f32[2,128,2,768]{3,1,2,0:T(8,128)S(1)} %fusion.20, f32[2,128,2,768]{3,1,2,0:T(8,128)S(1)} %fusion.22, f32[2,128,2,768]{3,1,2,0:T(8,128)S(1)} %fusion.24, f32[2,128,2,768]{3,1,2,0:T(8,128)S(1)} %fusion.26, f32[2,2,768,128]{2,3,1,0:T(8,128)S(1)} %fusion.30, ...), kind=kOutput, calls=%fused_computation.42 | convolution fusion | flops 310247424 | bytes 17018880 | tf_op jit(solution)/shard_map/hgrk,khd->rhgd/dot_general | solution.py:31
  (39 shorter events, 21.9 us)
Async XLA Ops:
  11.4 15.5 %all-to-all-start = ((bf16[8,96,256]{2,1,0:T(8,128)(2,1)}), bf16[8,96,256]{2,1,0:T(8,128)(2,1)S(1)}, u32[]{:S(2)}, u32[]{:S(2)}) async-start(bf16[8,96,256]{2,1,0:T(8,128)(2,1)} %bitcast_dynamic-update-slice_fusion), calls=%async_computation | async-start | bytes 786432 | tf_op jit(solution)/shard_map/all_to_all | solution.py:44
  26.9 15.2 %all-to-all-start.2 = ((bf16[96,8,256]{2,0,1:T(8,128)(2,1)}), bf16[96,8,256]{2,0,1:T(8,128)(2,1)S(1)}, u32[]{:S(2)}, u32[]{:S(2)}) async-start(bf16[96,8,256]{2,0,1:T(8,128)(2,1)} %bitcast.240), calls=%async_computation.2 | async-start | bytes 786432 | tf_op jit(solution)/shard_map/all_to_all | solution.py:47
  42.1 25.1 %all-to-all-start.1 = ((bf16[96,8,512]{2,0,1:T(8,128)(2,1)}), bf16[96,8,512]{2,0,1:T(8,128)(2,1)S(1)}, u32[]{:S(2)}, u32[]{:S(2)}) async-start(bf16[96,8,512]{2,0,1:T(8,128)(2,1)} %bitcast.239), calls=%async_computation.1 | async-start | bytes 1572864 | tf_op jit(solution)/shard_map/all_to_all | solution.py:42
  53.6 22.0 %collective-permute-start = (bf16[2,768,2,128]{3,1,2,0:T(8,128)(2,1)}, bf16[2,768,2,128]{3,1,2,0:T(8,128)(2,1)}, u32[]{:S(2)}, u32[]{:S(2)}) collective-permute-start(bf16[2,768,2,128]{3,1,2,0:T(8,128)(2,1)} %copy_dynamic-update-slice_fusion), channel_id=1, source_target_pairs={{0,1},{1,2},{2,3},{3,0},{4,5},{5,6},{6,7},{7,4},{8,9},{9,10},{10,1... | collective-permute-start | bytes 2359304 | tf_op jit(solution)/shard_map/while/body/eval_jaxpr/ppermute | solution.py:13
  55.9 23.2 %collective-permute-start.1 = (bf16[2,768,2,128]{3,1,2,0:T(8,128)(2,1)}, bf16[2,768,2,128]{3,1,2,0:T(8,128)(2,1)}, u32[]{:S(2)}, u32[]{:S(2)}) collective-permute-start(bf16[2,768,2,128]{3,1,2,0:T(8,128)(2,1)} %copy_dynamic-update-slice_fusion), channel_id=1, source_target_pairs={{0,3},{1,0},{2,1},{3,2},{4,7},{5,4},{6,5},{7,6},{8,11},{9,8},{10,9... | collective-permute-start | bytes 2359304 | tf_op jit(solution)/shard_map/while/body/eval_jaxpr/ppermute | solution.py:13
  67.4 2.8 %copy-start.3 = (pred[768,384]{0,1:T(8,128)(4,1)S(1)}, pred[768,384]{0,1:T(8,128)(4,1)}, u32[]{:S(2)}) copy-start(pred[768,384]{0,1:T(8,128)(4,1)} %get-tuple-element.46) | copy-start | bytes 884740
  70.2 1.8 %copy-start.2 = (pred[768,384]{0,1:T(8,128)(4,1)S(1)}, pred[768,384]{0,1:T(8,128)(4,1)}, u32[]{:S(2)}) copy-start(pred[768,384]{0,1:T(8,128)(4,1)} %get-tuple-element.28) | copy-start | bytes 884740
  73.8 5.3 %copy-start.1 = (pred[768,384]{0,1:T(8,128)(4,1)S(1)}, pred[768,384]{0,1:T(8,128)(4,1)}, u32[]{:S(2)}) copy-start(pred[768,384]{0,1:T(8,128)(4,1)} %get-tuple-element.44) | copy-start | bytes 884740
  75.6 24.8 %collective-permute-start.2 = (bf16[2,768,2,128]{3,1,2,0:T(8,128)(2,1)}, bf16[2,768,2,128]{3,1,2,0:T(8,128)(2,1)S(1)}, u32[]{:S(2)}, u32[]{:S(2)}) collective-permute-start(bf16[2,768,2,128]{3,1,2,0:T(8,128)(2,1)} %collective-permute-done), channel_id=1, source_target_pairs={{0,1},{1,2},{2,3},{3,0},{4,5},{5,6},{6,7},{7,4},{8,9},{9,10},{10,1... | collective-permute-start | bytes 2359304 | tf_op jit(solution)/shard_map/ppermute | solution.py:13
  81.8 2.6 %copy-start = (pred[768,384]{0,1:T(8,128)(4,1)S(1)}, pred[768,384]{0,1:T(8,128)(4,1)}, u32[]{:S(2)}) copy-start(pred[768,384]{0,1:T(8,128)(4,1)} %get-tuple-element.42) | copy-start | bytes 884740
